TPU v7x, 32 devices: a whole 2x2x4 slice. The times are simulated.
32 devices in a mesh: grp: 2 (over y), col: 4 (over z), row: 2 (over x), dir: 2 (over core).
Axes of the slice: x: 2, y: 2, z: 4, core: 2. Of those that a mesh axis runs over, the one named last changes fastest.
Arguments:
- slopes_in: bfloat16 [512, 8192], P(None, ('grp', 'col')), parts along dimension 1, may hold values from -6 to 6
- basis_left: bfloat16 [12, 16, 256, 256], P(('row', 'dir'), 'col'), may hold values from -0.09375 to 0.09375
- basis_right: bfloat16 [12, 16, 256, 256], P(('row', 'dir'), 'col'), may hold values from -0.375 to 0.375
- rank_blocks: int32 [12, 16], P(('row', 'dir'), 'col'), may hold values from 1 to 4
- tile_owner: int32 [16], replicated, may hold values from 0 to 15, each once
- footprint: int32 [4, 4, 4, 2048], P(('row', 'dir')), may hold values from 0 to 767
- trace_weight: float32 [4, 4, 4, 2048], P(('row', 'dir')), may hold values from 0 to 0.5
- fitting: bfloat16 [2048, 4096], P(None, 'col'), may hold values from -0.125 to 0.125
Outputs:
- commands: bfloat16 [4, 1024, 4096], P(('row', 'dir'), 'grp', 'col'), parts along dimension 1
There are 2 independent parts, one for each index of `grp`. A program takes and returns all parts, laid end to end along the dimension named above; an argument that names none is the same for every part. Nothing has to cross between parts.
Inputs may be any that keep to these rules, and one draw needn't show every extreme that they name: rank_blocks[i, k] is the number of leading blocks of 64 columns of tile (i, k) that are live. `tile_owner`: each slope block appears in exactly one tile slot. `footprint`: indices into one layer's points.
All inputs are finite; a program needn't handle non-finite values.
Results may differ from a plain program's by a relative error of at most 0.0064.
Values may be sent and summed in bfloat16 or wider, within the bound.
No kernel may reach another device: no remote copies, remote signals or barrier semaphores. Data moves between devices by JAX's collectives and lax.ppermute only.
A program may use at most 128 MiB of HBM per device.

v0:
```python
import jax
import jax.numpy as jnp
from jax import lax
from jax.sharding import PartitionSpec as P

RB = 64


def shards(
    slopes_in, basis_left, basis_right, rank_blocks, tile_owner, footprint, trace_weight, fitting
):
    frames = slopes_in.shape[0]
    tile_size = basis_left.shape[2]
    rows_here = basis_left.shape[0]
    slots_here = basis_left.shape[1]
    rank_cols = basis_left.shape[3]
    owners = lax.dynamic_slice_in_dim(tile_owner, lax.axis_index("col") * slots_here, slots_here, 0)
    share = frames // lax.axis_size(("row", "dir"))
    mine = lax.dynamic_slice_in_dim(slopes_in, lax.axis_index(("row", "dir")) * share, share, 0)
    partial_value = lax.all_gather(mine, "col", axis=1, tiled=True)
    picked = jnp.take(partial_value.reshape(share, -1, tile_size), owners, axis=1)
    chosen = lax.all_gather(picked, ("row", "dir"), axis=0, tiled=True)
    columns = jnp.arange(rank_cols, dtype=jnp.int32) // RB
    live = columns[None, None, None, :] < rank_blocks[:, :, None, None]
    frame_share = frames // lax.axis_size("col")
    coeffs = jnp.einsum("fkn,iknr->ikfr", chosen, basis_right, preferred_element_type=jnp.float32)
    coeffs = jnp.where(live, coeffs, 0.0).astype(jnp.bfloat16)
    summed = jnp.einsum("ikfr,iknr->fin", coeffs, basis_left, preferred_element_type=jnp.float32)
    layer_block = lax.psum_scatter(
        summed.reshape(lax.axis_size("col") * frame_share, rows_here * tile_size),
        "col",
        scatter_dimension=0,
        tiled=True,
    ).astype(jnp.bfloat16)
    layers = lax.all_gather(layer_block, ("row", "dir"), axis=1, tiled=True)
    layer_count = footprint.shape[1]
    pupil_count = footprint.shape[3]
    per_layer = layers.shape[1] // layer_count
    shifts = (jnp.arange(layer_count, dtype=jnp.int32) * per_layer)[:, None, None]
    flat = (footprint[0] + shifts).reshape(-1)
    values = (
        jnp.take(layers, flat, axis=1)
        .astype(jnp.float32)
        .reshape(frame_share, layer_count, 4, pupil_count)
    )
    pupil = jnp.sum(values * trace_weight[0][None], axis=(1, 2)).astype(jnp.bfloat16)
    commands = jnp.dot(
        lax.all_gather(pupil, "col", axis=0, tiled=True),
        fitting,
        preferred_element_type=jnp.float32,
    )
    return commands.astype(jnp.bfloat16)[None]


def solution(mesh):
    placed = (
        P(None, ("grp", "col")),
        P(("row", "dir"), "col", None, None),
        P(("row", "dir"), "col", None, None),
        P(("row", "dir"), "col"),
        P(),
        P(("row", "dir"), None, None, None),
        P(("row", "dir"), None, None, None),
        P(None, "col"),
    )
    return jax.shard_map(
        shards,
        mesh=mesh,
        in_specs=placed,
        out_specs=P(("row", "dir"), "grp", "col"),
        check_vma=False,
    )
```

profile of v0, /device:TPU:0, one launch (start us, length us, event | category | flops | bytes accessed | tf_op | source)
XLA Modules:
  0.0 293.8 jit_solution(6185712206535708235)
XLA Ops:
  6.5 0.0 copy-start
  6.5 0.0 all-gather.4.cloned.1.call-start
  6.6 1.1 constant_dynamic-slice_fusion
  7.7 0.8 copy.14
  8.5 0.0 all-gather.4.cloned.1.call-update
  8.5 0.0 all-gather.6.cloned.1.call-start
  8.6 0.7 compare_and_fusion.1
  9.3 30.3 %all-gather.4.cloned.1.call-done = bf16[128,4096]{0,1:T(8,128)(2,1)} async-done(((bf16[128,1024]{0,1:T(8,128)(2,1)}), bf16[128,4096]{0,1:T(8,128)(2,1)}) %all-gather.4.cloned.1.call-update) | async-done | bytes 1048592 | tf_op jit(solution)/shard_map/all_gather | solution.py:20
  39.6 1.5 copy.12
  41.1 0.6 gather_fusion
  41.7 0.8 select_bitcast_fusion
  42.5 0.0 all-gather.6.cloned.1.call-update
  42.5 0.0 reduce-scatter.2.cloned.1.call-start
  42.6 0.1 add.67
  42.7 0.2 add.75
  42.9 0.2 squeeze.6
  43.1 0.0 copy-done.3
  43.1 0.1 broadcast_compare_fusion
  43.1 15.6 %all-gather.6.cloned.1.call-done = bf16[512,4,256]{2,0,1:T(8,128)(2,1)} async-done(((bf16[128,4,256]{2,0,1:T(8,128)(2,1)}), bf16[512,4,256]{2,0,1:T(8,128)(2,1)}) %all-gather.6.cloned.1.call-update) | async-done | bytes 1048592 | tf_op jit(solution)/shard_map/all_gather | solution.py:22
  58.8 4.7 %fusion.1 = f32[3,512,256,1]{1,2,3,0:T(8,128)} fusion(bf16[3,4,256,256]{3,2,1,0:T(8,128)(2,1)S(1)} %copy-done, pred[3,4,256]{2,1,0:T(4,128)(4,1)S(1)} %broadcast_compare_fusion, bf16[3,4,256,256]{3,2,1,0:T(8,128)(2,1)} %param.10, bf16[512,4,256]{2,0,1:T(8,128)(2,1)} %all-gather.6.cloned.1.call-done), kind=kOutput, calls=%fused_computation.5 | convolution fusion | flops 1613758464 | bytes 5770240 | tf_op jit(solution)/shard_map/ikfr,iknr->fin/dot_general | solution.py:28
  63.4 0.0 reduce-scatter.2.cloned.1.call-update
  63.5 0.0 all-gather.8.cloned.1.call-start
  63.5 0.2 compare_select_fusion
  63.7 0.2 compare_and_fusion
  63.9 35.2 %reduce-scatter.2.cloned.1.call-done = f32[128,768]{0,1:T(8,128)} async-done(((f32[512,768]{0,1:T(8,128)}), f32[128,768]{0,1:T(8,128)}) %reduce-scatter.2.cloned.1.call-update) | async-done | bytes 393232 | tf_op jit(solution)/shard_map/reduce_scatter | solution.py:29
  99.1 1.0 convert_element_type.17
  100.1 8.6 %all_gather.14 = bf16[128,3072]{0,1:T(8,128)(2,1)S(1)} all-gather(bf16[128,768]{0,1:T(8,128)(2,1)S(1)} %convert_element_type.17), channel_id=1, replica_groups=mesh['grp'=2,'col'=4,'row'=2,'dir'=2] {'row','dir'}, dimensions={1}, use_global_device_ids=true | all-gather | bytes 983040 | tf_op jit(solution)/shard_map/all_gather | solution.py:35
  108.6 114.3 %gather_fusion.1 = bf16[32768,128]{1,0:T(8,128)(2,1)} fusion(bf16[128,3072]{0,1:T(8,128)(2,1)S(1)} %all_gather.14, s32[32768]{0:T(1024)S(1)} %broadcast_clamp_fusion), kind=kCustom, calls=%fused_computation.1 | custom fusion | bytes 16908288 | tf_op jit(solution)/shard_map/jit(_take)/gather | solution.py:42
  222.9 13.4 %multiply_reduce_fusion = bf16[128,2048]{0,1:T(8,128)(2,1)} fusion(f32[4,4,2048]{2,1,0:T(4,128)S(1)} %bitcast.39, bf16[128,4,4,2048]{0,3,2,1:T(8,128)(2,1)} %bitcast.35, pred[4,4,2048]{2,1,0:T(4,128)(4,1)S(1)} %compare_and_fusion), kind=kLoop, calls=%fused_computation.2 | loop fusion | flops 16515072 | bytes 9076736 | tf_op jit(solution)/shard_map/reduce_sum | solution.py:46
  236.3 0.0 all-gather.8.cloned.1.call-update
  236.3 44.8 %all-gather.8.cloned.1.call-done = bf16[512,2048]{0,1:T(8,128)(2,1)} async-done(((bf16[128,2048]{0,1:T(8,128)(2,1)}), bf16[512,2048]{0,1:T(8,128)(2,1)}) %all-gather.8.cloned.1.call-update) | async-done | bytes 2097168 | tf_op jit(solution)/shard_map/all_gather | solution.py:48
  281.2 6.1 %fusion.7 = bf16[1,512,1024]{2,1,0:T(8,128)(2,1)} fusion(bf16[512,2048]{0,1:T(8,128)(2,1)} %all-gather.8.cloned.1.call-done, bf16[2048,1024]{1,0:T(8,128)(2,1)} %param.15), kind=kOutput, calls=%fused_computation.10 | convolution fusion | flops 2148007936 | bytes 7340032 | tf_op jit(solution)/shard_map/dot_general | solution.py:47
  (10 shorter events, 0.0 us)
Async XLA Ops:
  6.5 52.2 %copy-start = (bf16[3,4,256,256]{3,2,1,0:T(8,128)(2,1)S(1)}, bf16[3,4,256,256]{3,2,1,0:T(8,128)(2,1)}, u32[]{:S(2)}) copy-start(bf16[3,4,256,256]{3,2,1,0:T(8,128)(2,1)} %param.9) | copy-start | bytes 4718596
  6.5 36.3 %copy-start.1 = (s32[1,4,4,2048]{3,2,1,0:T(4,128)S(1)}, s32[1,4,4,2048]{3,2,1,0:T(4,128)}, u32[]{:S(2)}) copy-start(s32[1,4,4,2048]{3,2,1,0:T(4,128)} %param.13) | copy-start | bytes 393220
  6.5 36.5 %copy-start.3 = (s32[3,4]{1,0:T(4,128)S(1)}, s32[3,4]{1,0:T(4,128)}, u32[]{:S(2)}) copy-start(s32[3,4]{1,0:T(4,128)} %param.11) | copy-start | bytes 148
  6.5 33.1 %all-gather.4.cloned.1.call-start = ((), (), s32[]{:S(2)}) async-start(), calls=%async_computation.1 | async-start | bytes 1310720 | tf_op jit(solution)/shard_map/all_gather | solution.py:20
  8.5 50.2 %all-gather.6.cloned.1.call-start = ((), (), s32[]{:S(2)}) async-start(), calls=%async_computation.2 | async-start | bytes 1310720 | tf_op jit(solution)/shard_map/all_gather | solution.py:22
  42.5 56.5 %reduce-scatter.2.cloned.1.call-start = ((), (), s32[]{:S(2)}) async-start(), calls=%async_computation.3 | async-start | bytes 1966080 | tf_op jit(solution)/shard_map/reduce_scatter | solution.py:29
  63.5 217.7 %all-gather.8.cloned.1.call-start = ((), (), s32[]{:S(2)}) async-start(), calls=%async_computation.4 | async-start | bytes 2621440 | tf_op jit(solution)/shard_map/all_gather | solution.py:48
  108.6 114.3 %copy-start.2 = (f32[1,4,4,2048]{3,2,1,0:T(4,128)S(1)}, f32[1,4,4,2048]{3,2,1,0:T(4,128)}, u32[]{:S(2)}) copy-start(f32[1,4,4,2048]{3,2,1,0:T(4,128)} %param.14) | copy-start | bytes 393220
Sparse Core Ops, SparseCore 0:
  8.9 30.6 all-gather.3
  42.6 16.0 all-gather.5
  63.6 35.4 reduce-scatter.1
  236.5 44.6 all-gather.7
where the time goes:
time: 294 us
  waiting for transfers between devices  126 us (43%)
  local copies, waits for them, and re-layouts  119 us (40%)
  other arithmetic  16.4 us (6%)
  between operations  13.2 us (4%)
  matrix products  10.8 us (4%)
  blocking collectives  8.58 us (3%)
    gather x1, local copies, waits for them, and re-layouts, shards(): jnp.take(layers, flat, axis=1).astype(jnp.float32)  114 us
    all_gather x1, waiting for transfers between devices, shards(): lax.all_gather(pupil, 'col', axis=0, tiled=True)  44.8 us
    reduce_scatter x1, waiting for transfers between devices, shards(): lax.psum_scatter(summed.reshape(lax.axis_size('col') * frame_share, rows_...  35.2 us
    all_gather x1, waiting for transfers between devices, shards(): partial_value = lax.all_gather(mine, 'col', axis=1, tiled=True)  30.3 us
    all_gather x1, waiting for transfers between devices, shards(): chosen = lax.all_gather(picked, ('row', 'dir'), axis=0, tiled=True)  15.6 us
    reduce_sum x1, other arithmetic, shards(): jnp.sum(values * trace_weight[0][None], axis=(1, 2)).astype(jnp.bfloat16)  13.4 us
    all_gather x1, blocking collectives, shards(): layers = lax.all_gather(layer_block, ('row', 'dir'), axis=1, tiled=True)  8.58 us
    dot_general x1, matrix products, shards(): jnp.dot(lax.all_gather(pupil, 'col', axis=0, tiled=True), fitting, prefer...  6.14 us
  transfers between devices with their start and end apart: 4, of which 4 were waited for; matrix products, arithmetic and copies ran while one was open for 1% of the time, Pallas kernels for 0%

commit v1 on v0

--- a/solution.py
+++ b/solution.py
@@ -4,6 +4,16 @@
 from jax.sharding import PartitionSpec as P
 
 RB = 64
+
+
+def scales_assign(block_in, axis_no):
+    block_in = jnp.moveaxis(block_in, 0, axis_no)
+    block_next = block_in.shape
+    return block_in.reshape(
+        *block_next[:axis_no],
+        block_next[axis_no] * block_next[axis_no + 1],
+        *block_next[axis_no + 2 :]
+    )
 
 
 def shards(
@@ -19,11 +29,27 @@
     mine = lax.dynamic_slice_in_dim(slopes_in, lax.axis_index(("row", "dir")) * share, share, 0)
     partial_value = lax.all_gather(mine, "col", axis=1, tiled=True)
     picked = jnp.take(partial_value.reshape(share, -1, tile_size), owners, axis=1)
-    chosen = lax.all_gather(picked, ("row", "dir"), axis=0, tiled=True)
     columns = jnp.arange(rank_cols, dtype=jnp.int32) // RB
     live = columns[None, None, None, :] < rank_blocks[:, :, None, None]
     frame_share = frames // lax.axis_size("col")
-    coeffs = jnp.einsum("fkn,iknr->ikfr", chosen, basis_right, preferred_element_type=jnp.float32)
+    z_new, top, out_arr = (
+        lax.axis_size(("row", "dir")),
+        lax.axis_index(("row", "dir")),
+        picked.shape[0],
+    )
+    cards = []
+    for hop_no in range(z_new):
+        cards.append((hop_no, (hop_no + 1) % z_new))
+    store = []
+    z1 = picked
+    for pp in range(z_new):
+        u_next = z1 if pp == z_new - 1 else lax.ppermute(z1, perm=cards, axis_name=("row", "dir"))
+        store.append(
+            jnp.einsum("fkn,iknr->ikfr", z1, basis_right, preferred_element_type=jnp.float32)
+        )
+        z1 = u_next
+    store = jnp.stack(store, axis=0)[(top - jnp.arange(z_new)) % z_new]
+    coeffs = scales_assign(store, 2)
     coeffs = jnp.where(live, coeffs, 0.0).astype(jnp.bfloat16)
     summed = jnp.einsum("ikfr,iknr->fin", coeffs, basis_left, preferred_element_type=jnp.float32)
     layer_block = lax.psum_scatter(

time: 294 us -> 302 us (1.027)
  local copies, waits for them, and re-layouts: 119 us -> 127 us
    all_gather x1 -> x0, waiting for transfers between devices: 15.6 us -> none  [shards(): chosen = lax.all_gather(picked, ('row', 'dir'), axis=0, tiled=True)]
    ppermute x0 -> x3, waiting for transfers between devices: none -> 15.6 us  [shards(): lax.ppermute(z1, perm=cards, axis_name=('row', 'dir'))]
    gather x0 -> x1, local copies, waits for them, and re-layouts: none -> 4.31 us  [shards(): store = jnp.stack(store, axis=0)[(top - jnp.arange(z_new)) % z_new]]
  transfers between devices with their start and end apart: 4 -> 6, of which waited for: 4 -> 6; matrix products, arithmetic and copies ran while one was open for 1% -> 1% of each run, Pallas kernels for 0% -> 0%
where the time goes in v1:
time: 302 us
  local copies, waits for them, and re-layouts  127 us (42%)
  waiting for transfers between devices  125 us (41%)
  other arithmetic  18.4 us (6%)
  between operations  13.3 us (4%)
  matrix products  9.88 us (3%)
  blocking collectives  8.58 us (3%)
    gather x1, local copies, waits for them, and re-layouts, shards(): jnp.take(layers, flat, axis=1).astype(jnp.float32)  115 us
    all_gather x1, waiting for transfers between devices, shards(): lax.all_gather(pupil, 'col', axis=0, tiled=True)  44.8 us
    reduce_scatter x1, waiting for transfers between devices, shards(): lax.psum_scatter(summed.reshape(lax.axis_size('col') * frame_share, rows_...  34.5 us
    all_gather x1, waiting for transfers between devices, shards(): partial_value = lax.all_gather(mine, 'col', axis=1, tiled=True)  30.3 us
    ppermute x3, waiting for transfers between devices, shards(): lax.ppermute(z1, perm=cards, axis_name=('row', 'dir'))  15.6 us
    reduce_sum x1, other arithmetic, shards(): jnp.sum(values * trace_weight[0][None], axis=(1, 2)).astype(jnp.bfloat16)  13.4 us
    all_gather x1, blocking collectives, shards(): layers = lax.all_gather(layer_block, ('row', 'dir'), axis=1, tiled=True)  8.58 us
    dot_general x1, matrix products, shards(): jnp.dot(lax.all_gather(pupil, 'col', axis=0, tiled=True), fitting, prefer...  6.14 us
  transfers between devices with their start and end apart: 6, of which 6 were waited for; matrix products, arithmetic and copies ran while one was open for 1% of the time, Pallas kernels for 0%

profile of v1, /device:TPU:0, one launch (start us, length us, event | category | flops | bytes accessed | tf_op | source)
XLA Modules:
  0.0 302.1 jit_solution(14214362011150699467)
XLA Ops:
  6.6 1.1 constant_dynamic-slice_fusion
  7.7 0.8 copy.37
  8.6 0.7 compare_and_fusion.1
  9.4 30.3 %all-gather.3.cloned.1.call-done = bf16[128,4096]{0,1:T(8,128)(2,1)} async-done(((bf16[128,1024]{0,1:T(8,128)(2,1)}), bf16[128,4096]{0,1:T(8,128)(2,1)}) %all-gather.3.cloned.1.call-update) | async-done | bytes 1048592 | tf_op jit(solution)/shard_map/all_gather | solution.py:30
  39.6 1.5 copy.26
  41.1 0.6 gather_fusion
  41.7 0.1 fusion.10
  42.0 5.7 %collective-permute-done = bf16[128,4,256]{2,0,1:T(8,128)(2,1)S(1)} collective-permute-done((bf16[128,4,256]{2,0,1:T(8,128)(2,1)S(1)}, bf16[128,4,256]{2,0,1:T(8,128)(2,1)S(1)}, u32[]{:S(2)}, u32[]{:S(2)}) %collective-permute-start) | collective-permute-done | bytes 262176 | tf_op jit(solution)/shard_map/ppermute | solution.py:46
  47.7 0.1 add.91
  47.8 0.2 add.101
  47.9 0.2 squeeze.6
  48.1 0.4 convolution_bitcast_fusion.3
  48.5 4.9 %collective-permute-done.1 = bf16[128,4,256]{2,0,1:T(8,128)(2,1)S(1)} collective-permute-done((bf16[128,4,256]{2,0,1:T(8,128)(2,1)S(1)}, bf16[128,4,256]{2,0,1:T(8,128)(2,1)S(1)}, u32[]{:S(2)}, u32[]{:S(2)}) %collective-permute-start.1) | collective-permute-done | bytes 262176 | tf_op jit(solution)/shard_map/ppermute | solution.py:46
  53.5 0.4 convolution_bitcast_fusion.2
  53.8 0.4 convolution_bitcast_fusion.1
  54.2 5.0 %collective-permute-done.2 = bf16[128,4,256]{2,0,1:T(8,128)(2,1)S(1)} collective-permute-done((bf16[128,4,256]{2,0,1:T(8,128)(2,1)S(1)}, bf16[128,4,256]{2,0,1:T(8,128)(2,1)S(1)}, u32[]{:S(2)}, u32[]{:S(2)}) %collective-permute-start.2) | collective-permute-done | bytes 262176 | tf_op jit(solution)/shard_map/ppermute | solution.py:46
  59.2 0.4 convolution_bitcast_fusion
  59.6 1.9 pad_maximum_fusion
  61.5 4.3 %gather_fusion.1 = bf16[4,3,4,128,256]{4,3,1,2,0:T(8,128)(2,1)} fusion(bf16[4,3,4,128,256]{4,3,1,2,0:T(8,128)(2,1)} %pad_maximum_fusion, s32[1024]{0:T(1024)S(1)} %pad_clamp_fusion), kind=kCustom, calls=%fused_computation.1 | custom fusion | bytes 6291472 | tf_op jit(solution)/shard_map/gather | solution.py:51
  65.8 2.2 copy.31
  68.1 0.8 fusion
  68.8 0.6 copy-done.1
  69.5 2.2 fusion.14
  71.7 0.2 compare_select_fusion
  71.9 0.2 compare_and_fusion
  72.1 34.5 %reduce-scatter.2.cloned.1.call-done = f32[128,768]{0,1:T(8,128)} async-done(((f32[512,768]{0,1:T(8,128)}), f32[128,768]{0,1:T(8,128)}) %reduce-scatter.2.cloned.1.call-update) | async-done | bytes 393232 | tf_op jit(solution)/shard_map/reduce_scatter | solution.py:55
  106.6 1.0 convert_element_type.17
  107.6 8.6 %all_gather.10 = bf16[128,3072]{0,1:T(8,128)(2,1)S(1)} all-gather(bf16[128,768]{0,1:T(8,128)(2,1)S(1)} %convert_element_type.17), channel_id=1, replica_groups=mesh['grp'=2,'col'=4,'row'=2,'dir'=2] {'row','dir'}, dimensions={1}, use_global_device_ids=true | all-gather | bytes 983040 | tf_op jit(solution)/shard_map/all_gather | solution.py:61
  116.2 115.0 %gather_fusion.2 = bf16[32768,128]{1,0:T(8,128)(2,1)} fusion(bf16[128,3072]{0,1:T(8,128)(2,1)S(1)} %all_gather.10, s32[32768]{0:T(1024)S(1)} %broadcast_clamp_fusion), kind=kCustom, calls=%fused_computation.2 | custom fusion | bytes 16908288 | tf_op jit(solution)/shard_map/jit(_take)/gather | solution.py:68
  231.2 13.4 %multiply_reduce_fusion = bf16[128,2048]{0,1:T(8,128)(2,1)} fusion(f32[4,4,2048]{2,1,0:T(4,128)S(1)} %bitcast.75, bf16[128,4,4,2048]{0,3,2,1:T(8,128)(2,1)} %bitcast.70, pred[4,4,2048]{2,1,0:T(4,128)(4,1)S(1)} %compare_and_fusion), kind=kLoop, calls=%fused_computation.3 | loop fusion | flops 16515072 | bytes 9076736 | tf_op jit(solution)/shard_map/reduce_sum | solution.py:72
  244.6 44.8 %all-gather.5.cloned.1.call-done = bf16[512,2048]{0,1:T(8,128)(2,1)} async-done(((bf16[128,2048]{0,1:T(8,128)(2,1)}), bf16[512,2048]{0,1:T(8,128)(2,1)}) %all-gather.5.cloned.1.call-update) | async-done | bytes 2097168 | tf_op jit(solution)/shard_map/all_gather | solution.py:74
  289.5 6.1 %fusion.1 = bf16[1,512,1024]{2,1,0:T(8,128)(2,1)} fusion(bf16[512,2048]{0,1:T(8,128)(2,1)} %all-gather.5.cloned.1.call-done, bf16[2048,1024]{1,0:T(8,128)(2,1)} %param.15), kind=kOutput, calls=%fused_computation.12 | convolution fusion | flops 2148007936 | bytes 7340032 | tf_op jit(solution)/shard_map/dot_general | solution.py:73
  (25 shorter events, 0.3 us)
Async XLA Ops:
  6.5 41.6 %copy-start = (bf16[3,4,256,256]{3,2,1,0:T(8,128)(2,1)S(1)}, bf16[3,4,256,256]{3,2,1,0:T(8,128)(2,1)}, u32[]{:S(2)}) copy-start(bf16[3,4,256,256]{3,2,1,0:T(8,128)(2,1)} %param.10) | copy-start | bytes 4718596
  6.5 35.3 %copy-start.4 = (s32[3,4]{1,0:T(4,128)S(1)}, s32[3,4]{1,0:T(4,128)}, u32[]{:S(2)}) copy-start(s32[3,4]{1,0:T(4,128)} %param.11) | copy-start | bytes 148
  6.5 41.4 %copy-start.2 = (s32[1,4,4,2048]{3,2,1,0:T(4,128)S(1)}, s32[1,4,4,2048]{3,2,1,0:T(4,128)}, u32[]{:S(2)}) copy-start(s32[1,4,4,2048]{3,2,1,0:T(4,128)} %param.13) | copy-start | bytes 393220
  6.5 33.1 %all-gather.3.cloned.1.call-start = ((), (), s32[]{:S(2)}) async-start(), calls=%async_computation.1 | async-start | bytes 1310720 | tf_op jit(solution)/shard_map/all_gather | solution.py:30
  8.5 98.1 %reduce-scatter.2.cloned.1.call-start = ((), (), s32[]{:S(2)}) async-start(), calls=%async_computation.2 | async-start | bytes 1966080 | tf_op jit(solution)/shard_map/reduce_scatter | solution.py:55
  41.8 5.8 %collective-permute-start = (bf16[128,4,256]{2,0,1:T(8,128)(2,1)S(1)}, bf16[128,4,256]{2,0,1:T(8,128)(2,1)S(1)}, u32[]{:S(2)}, u32[]{:S(2)}) collective-permute-start(bf16[128,4,256]{2,0,1:T(8,128)(2,1)S(1)} %fusion.10), channel_id=1, source_target_pairs={{0,1},{1,2},{2,3},{3,0},{4,5},{5,6},{6,7},{7,4},{8,9},{9,10},{10,1... | collective-permute-start | bytes 786440 | tf_op jit(solution)/shard_map/ppermute | solution.py:46
  47.7 5.8 %collective-permute-start.1 = (bf16[128,4,256]{2,0,1:T(8,128)(2,1)S(1)}, bf16[128,4,256]{2,0,1:T(8,128)(2,1)S(1)}, u32[]{:S(2)}, u32[]{:S(2)}) collective-permute-start(bf16[128,4,256]{2,0,1:T(8,128)(2,1)S(1)} %collective-permute-done), channel_id=1, source_target_pairs={{0,1},{1,2},{2,3},{3,0},{4,5},{5,6},{6,7},{7,4},{8,9},{9,10},{10,1... | collective-permute-start | bytes 786440 | tf_op jit(solution)/shard_map/ppermute | solution.py:46
  53.5 5.8 %collective-permute-start.2 = (bf16[128,4,256]{2,0,1:T(8,128)(2,1)S(1)}, bf16[128,4,256]{2,0,1:T(8,128)(2,1)S(1)}, u32[]{:S(2)}, u32[]{:S(2)}) collective-permute-start(bf16[128,4,256]{2,0,1:T(8,128)(2,1)S(1)} %collective-permute-done.1), channel_id=1, source_target_pairs={{0,1},{1,2},{2,3},{3,0},{4,5},{5,6},{6,7},{7,4},{8,9},{9,10},{10,1... | collective-permute-start | bytes 786440 | tf_op jit(solution)/shard_map/ppermute | solution.py:46
  68.0 1.4 copy-start.1
  71.7 217.8 %all-gather.5.cloned.1.call-start = ((), (), s32[]{:S(2)}) async-start(), calls=%async_computation.3 | async-start | bytes 2621440 | tf_op jit(solution)/shard_map/all_gather | solution.py:74
  116.2 115.0 %copy-start.3 = (f32[1,4,4,2048]{3,2,1,0:T(4,128)S(1)}, f32[1,4,4,2048]{3,2,1,0:T(4,128)}, u32[]{:S(2)}) copy-start(f32[1,4,4,2048]{3,2,1,0:T(4,128)} %param.14) | copy-start | bytes 393220
Sparse Core Ops, SparseCore 0:
  8.9 30.6 all-gather.2
  71.8 34.8 reduce-scatter.1
  244.8 44.6 all-gather.4
